TPU v7x, 256 devices: a whole 4x4x8 slice. The times are simulated.
256 devices in a mesh: shard: 64 (over z, x, core), model: 4 (over y).
Axes of the slice: x: 4, y: 4, z: 8, core: 2. Of those that a mesh axis runs over, the one named last changes fastest.
Arguments:
- grad_stack: float32 [512, 128, 2048], P(None, 'shard', 'model'), may hold values from -6 to 6
- moment_stack: float32 [512, 128, 2048], P(None, 'shard', 'model'), may hold values from -6 to 6
- weight_stack: float32 [512, 128, 2048], P(None, 'shard', 'model'), may hold values from -0.1875 to 0.1875
Outputs:
- new_weights: float32 [512, 128, 2048], P(None, 'shard', 'model')
- new_momentum: float32 [512, 128, 2048], P(None, 'shard', 'model')
All inputs are finite; a program needn't handle non-finite values.
Results may differ from a plain program's by a relative error of at most 0.00021.
Values sent between devices are 32-bit elements; how exact they have to be, the bound alone decides.
A program may use at most 64 MiB of HBM per device.

v0:
```python
import jax
import jax.numpy as jnp
from jax import lax
from jax.sharding import PartitionSpec as P

hold_rate = 0.95
learn_rate = 1.0
decay_rate = 0.1
HIGH = lax.Precision.HIGHEST


def mul(a, b):
    return jnp.einsum("mij,mjk->mik", a, b, precision=HIGH)


def chain(gram, steps):
    eye = jnp.eye(gram.shape[-1], dtype=gram.dtype)
    total = None
    for step in range(steps):
        factor = 3.4445 * eye - 4.775 * gram + 2.0315 * mul(gram, gram)
        total = factor if total is None else mul(factor, total)
        if step < steps - 1:
            gram = mul(mul(factor, gram), factor)
    return total


def summed_gram(rows):
    part = jnp.einsum("mik,mjk->mij", rows, rows, precision=HIGH)
    parts = lax.all_to_all(part, "model", split_axis=0, concat_axis=0, tiled=True)
    return parts.reshape(4, -1, *parts.shape[1:]).sum(axis=0)


def on_device(grad_stack, moment_stack, weight_stack):
    new_momentum = hold_rate * moment_stack + grad_stack
    rows = lax.all_to_all(new_momentum, "shard", split_axis=0, concat_axis=1, tiled=True)
    gram = summed_gram(rows)
    scale = lax.rsqrt(jnp.trace(gram, axis1=1, axis2=2)[:, None, None] + 1e-06)
    first = chain(gram * scale * scale, 2) * scale
    rows = mul(lax.all_gather(first, "model", axis=0, tiled=True), rows)
    second = chain(summed_gram(rows), 3)
    rows = mul(lax.all_gather(second, "model", axis=0, tiled=True), rows)
    back = lax.all_to_all(rows, "shard", split_axis=1, concat_axis=0, tiled=True)
    new_weights = (1.0 - learn_rate * decay_rate) * weight_stack - learn_rate * back
    return (new_weights, new_momentum)


def solution(mesh):
    spec = P(None, "shard", "model")
    return jax.shard_map(
        on_device, mesh=mesh, in_specs=(spec,) * 3, out_specs=(spec,) * 2, check_vma=False
    )
```

profile of v0, /device:TPU:2, one launch (start us, length us, event | category | flops | bytes accessed | tf_op | source)
XLA Modules:
  0.0 198.5 jit_solution(3235271127646908158)
XLA Ops:
  0.6 3.7 %multiply_add_fusion = f32[512,2,512]{2,1,0:T(2,128)S(1)} fusion(f32[512,2,512]{2,1,0:T(2,128)} %param.3, f32[512,2,512]{2,1,0:T(2,128)} %param.4), kind=kLoop, calls=%fused_computation.2 | loop fusion | flops 1048576 | bytes 6291456 | tf_op jit(solution)/shard_map/add | solution.py:34
  4.3 63.1 %all_to_all.46 = f32[512,2,512]{2,1,0:T(2,128)S(1)} all-to-all(f32[512,2,512]{2,1,0:T(2,128)S(1)} %multiply_add_fusion), channel_id=1, replica_groups=mesh['shard'=64,'model'=4] {'shard'}, dimensions={0} | all-to-all | bytes 4194304 | tf_op jit(solution)/shard_map/all_to_all | solution.py:35
  67.4 2.1 %copy.11 = f32[64,8,2,512]{3,2,0,1:T(2,128)} copy(f32[64,8,2,512]{3,2,1,0:T(2,128)S(1)} %bitcast.46) | data formatting | bytes 4194304 | tf_op jit(solution)/shard_map/all_to_all | solution.py:35
  69.4 2.7 %all_to_all.35 = f32[8,128,512]{2,1,0:T(8,128)S(1)} reshape(f32[8,64,2,512]{3,2,1,0:T(2,128)} %bitcast.44) | data formatting | bytes 4194304 | tf_op jit(solution)/shard_map/all_to_all | solution.py:35
  72.1 2.9 %fusion.8 = f32[8,128,128]{2,1,0:T(8,128)} fusion(f32[8,128,512]{2,1,0:T(8,128)S(1)} %all_to_all.35), kind=kOutput, calls=%fused_computation.22 | convolution fusion | flops 805306368 | bytes 2621440 | tf_op jit(solution)/shard_map/mik,mjk->mij/dot_general | solution.py:28
  75.0 4.5 %all-to-all-start.1 = ((f32[8,128,128]{2,1,0:T(8,128)}), f32[8,128,128]{2,1,0:T(8,128)S(1)}, u32[]{:S(2)}, u32[]{:S(2)}) async-start(f32[8,128,128]{2,1,0:T(8,128)} %fusion.8), calls=%async_computation.1 | async-start | bytes 1048576 | tf_op jit(solution)/shard_map/all_to_all | solution.py:29
  79.5 8.0 %all-to-all-done.1 = f32[8,128,128]{2,1,0:T(8,128)S(1)} async-done(((f32[8,128,128]{2,1,0:T(8,128)}), f32[8,128,128]{2,1,0:T(8,128)S(1)}, u32[]{:S(2)}, u32[]{:S(2)}) %all-to-all-start.1) | async-done | bytes 524320 | tf_op jit(solution)/shard_map/all_to_all | solution.py:29
  87.6 0.1 select_reduce_fusion
  87.7 0.4 fusion.4
  88.1 0.3 fusion.5
  88.4 0.3 fusion.9
  88.7 0.3 fusion.3
  89.0 0.3 convolution_multiply_fusion.3
  89.2 12.8 %all_gather.6 = f32[8,128,128]{2,1,0:T(8,128)S(1)} all-gather(f32[2,128,128]{2,1,0:T(8,128)S(1)} %convolution_multiply_fusion.3), channel_id=1, replica_groups=mesh['shard'=64,'model'=4] {'model'}, dimensions={0}, use_global_device_ids=true | all-gather | bytes 655360 | tf_op jit(solution)/shard_map/all_gather | solution.py:39
  102.0 1.8 fusion.10
  103.9 2.1 %fusion.11 = f32[8,128,128]{2,1,0:T(8,128)S(1)} fusion(f32[8,128,512]{2,1,0:T(8,128)S(1)} %fusion.10), kind=kOutput, calls=%fused_computation.25 | convolution fusion | flops 805306368 | bytes 2621440 | tf_op jit(solution)/shard_map/mik,mjk->mij/dot_general | solution.py:28
  106.0 11.3 %all_to_all.47 = f32[8,128,128]{2,1,0:T(8,128)S(1)} all-to-all(f32[8,128,128]{2,1,0:T(8,128)S(1)} %fusion.11), channel_id=1, replica_groups=mesh['shard'=64,'model'=4] {'model'}, dimensions={0} | all-to-all | bytes 1048576 | tf_op jit(solution)/shard_map/all_to_all | solution.py:29
  117.4 0.3 fusion.2
  117.6 0.3 fusion.12
  117.9 0.3 fusion.13
  118.2 0.3 fusion.1
  118.5 0.3 fusion.16
  118.7 0.3 fusion.14
  119.0 0.3 fusion.15
  119.3 0.3 fusion
  119.6 0.3 fusion.17
  119.8 12.8 %all_gather.7 = f32[8,128,128]{2,1,0:T(8,128)S(1)} all-gather(f32[2,128,128]{2,1,0:T(8,128)S(1)} %fusion.17), channel_id=1, replica_groups=mesh['shard'=64,'model'=4] {'model'}, dimensions={0}, use_global_device_ids=true | all-gather | bytes 655360 | tf_op jit(solution)/shard_map/all_gather | solution.py:41
  132.6 1.8 fusion.18
  134.5 1.2 copy.8
  135.7 57.6 %all_to_all.48 = f32[8,128,512]{2,0,1:T(8,128)S(1)} all-to-all(f32[8,128,512]{2,0,1:T(8,128)S(1)} %copy.8), channel_id=1, replica_groups=mesh['shard'=64,'model'=4] {'shard'}, dimensions={1} | all-to-all | bytes 4194304 | tf_op jit(solution)/shard_map/all_to_all | solution.py:42
  193.3 1.9 copy.9
  195.3 3.3 %bitcast_subtract_fusion = f32[512,2,512]{2,1,0:T(2,128)} fusion(f32[64,8,2,512]{3,2,1,0:T(2,128)S(1)} %copy.9, f32[512,2,512]{2,1,0:T(2,128)S(1)} %copy-done.3), kind=kLoop, calls=%fused_computation | loop fusion | flops 1048576 | bytes 6291456 | tf_op jit(solution)/shard_map/sub | solution.py:43
  (13 shorter events, 0.1 us)
Async XLA Ops:
  4.3 63.1 %copy-start.2 = (f32[512,2,512]{2,1,0:T(2,128)}, f32[512,2,512]{2,1,0:T(2,128)S(1)}, u32[]{:S(2)}) copy-start(f32[512,2,512]{2,1,0:T(2,128)S(1)} %multiply_add_fusion) | copy-start | bytes 6291460
  75.0 12.5 %all-to-all-start.1 = ((f32[8,128,128]{2,1,0:T(8,128)}), f32[8,128,128]{2,1,0:T(8,128)S(1)}, u32[]{:S(2)}, u32[]{:S(2)}) async-start(f32[8,128,128]{2,1,0:T(8,128)} %fusion.8), calls=%async_computation.1 | async-start | bytes 1048576 | tf_op jit(solution)/shard_map/all_to_all | solution.py:29
  103.9 2.1 %copy-start = (f32[8,128,512]{2,1,0:T(8,128)}, f32[8,128,512]{2,1,0:T(8,128)S(1)}, u32[]{:S(2)}) copy-start(f32[8,128,512]{2,1,0:T(8,128)S(1)} %fusion.10) | copy-start | bytes 6291460
  117.3 15.3 %copy-start.1 = (f32[8,128,512]{2,1,0:T(8,128)S(1)}, f32[8,128,512]{2,1,0:T(8,128)}, u32[]{:S(2)}) copy-start(f32[8,128,512]{2,1,0:T(8,128)} %copy-done) | copy-start | bytes 6291460
  193.3 1.9 copy-start.3
where the time goes:
time: 199 us
  blocking collectives  158 us (79%)
  matrix products  12.5 us (6%)
  waiting for transfers between devices  8.05 us (4%)
  local copies, waits for them, and re-layouts  7.95 us (4%)
  other arithmetic  7.12 us (4%)
  starting transfers between devices  4.46 us (2%)
    all_to_all x1, blocking collectives, on_device(): lax.all_to_all(new_momentum, 'shard', split_axis=0, concat_axis=1, tiled=...  63.1 us
    all_to_all x1, blocking collectives, on_device(): lax.all_to_all(rows, 'shard', split_axis=1, concat_axis=0, tiled=True)  57.6 us
    all_gather x1, blocking collectives, on_device(): rows = mul(lax.all_gather(first, 'model', axis=0, tiled=True), rows)  12.8 us
    all_gather x1, blocking collectives, on_device(): rows = mul(lax.all_gather(second, 'model', axis=0, tiled=True), rows)  12.8 us
    all_to_all x1, blocking collectives, summed_gram(): lax.all_to_all(part, 'model', split_axis=0, concat_axis=0, tiled=True)  11.3 us
    all_to_all x1, waiting for transfers between devices, summed_gram(): lax.all_to_all(part, 'model', split_axis=0, concat_axis=0, tiled=True)  8.05 us
    dot_general x16, matrix products, mul(): return jnp.einsum('mij,mjk->mik', a, b, precision=HIGH)  7.6 us
    dot_general x2, matrix products, summed_gram(): part = jnp.einsum('mik,mjk->mij', rows, rows, precision=HIGH)  4.93 us
  transfers between devices with their start and end apart: 1, of which 1 were waited for; matrix products, arithmetic and copies ran while one was open for 0% of the time, Pallas kernels for 0%

commit v1 on v0

--- a/solution.py
+++ b/solution.py
@@ -7,6 +7,24 @@
 learn_rate = 1.0
 decay_rate = 0.1
 HIGH = lax.Precision.HIGHEST
+
+
+def ring_gather(shard, axis, dim):
+    ways, here, lap = (lax.axis_size(axis), lax.axis_index(axis), shard.shape[dim])
+    shape = [n * ways if d == dim else n for d, n in enumerate(shard.shape)]
+    full = lax.dynamic_update_slice_in_dim(
+        jnp.zeros(shape, shard.dtype), shard, here * lap, axis=dim
+    )
+    going_up = going_down = shard
+    for far in range(1, ways // 2 + 1):
+        going_up = lax.ppermute(going_up, axis, [(d, (d + 1) % ways) for d in range(ways)])
+        full = lax.dynamic_update_slice_in_dim(full, going_up, (here - far) % ways * lap, axis=dim)
+        if 2 * far < ways:
+            going_down = lax.ppermute(going_down, axis, [(d, (d - 1) % ways) for d in range(ways)])
+            full = lax.dynamic_update_slice_in_dim(
+                full, going_down, (here + far) % ways * lap, axis=dim
+            )
+    return full
 
 
 def mul(a, b):
@@ -38,7 +56,7 @@
     first = chain(gram * scale * scale, 2) * scale
     rows = mul(lax.all_gather(first, "model", axis=0, tiled=True), rows)
     second = chain(summed_gram(rows), 3)
-    rows = mul(lax.all_gather(second, "model", axis=0, tiled=True), rows)
+    rows = mul(ring_gather(second, "model", 0), rows)
     back = lax.all_to_all(rows, "shard", split_axis=1, concat_axis=0, tiled=True)
     new_weights = (1.0 - learn_rate * decay_rate) * weight_stack - learn_rate * back
     return (new_weights, new_momentum)

time: 199 us -> 201 us (1.010)
  blocking collectives: 158 us -> 133 us
  waiting for transfers between devices: 8.05 us -> 26.3 us
  starting transfers between devices: 4.46 us -> 11.4 us
    all_gather x1 -> x0, blocking collectives: 12.8 us -> none  [on_device(): rows = mul(lax.all_gather(second, 'model', axis=0, tiled=True), rows)]
    all_to_all x1 -> x0, blocking collectives: 11.3 us -> none  [summed_gram(): lax.all_to_all(part, 'model', split_axis=0, concat_axis=0, tiled=True)]
    all_to_all x1 -> x2, waiting for transfers between devices: 8.05 us -> 17.2 us  [summed_gram(): lax.all_to_all(part, 'model', split_axis=0, concat_axis=0, tiled=True)]
    ppermute x0 -> x3, waiting for transfers between devices: none -> 9.07 us  [the longest x2 9.07 us: ring_gather(): lax.ppermute(going_up, axis, [(d, (d + 1) % ways) for d in range(ways)])]
    all_to_all x1 -> x2, starting transfers between devices: 4.46 us -> 8.12 us  [summed_gram(): lax.all_to_all(part, 'model', split_axis=0, concat_axis=0, tiled=True)]
    ppermute x0 -> x3, starting transfers between devices: none -> 3.31 us  [the longest x1 3.22 us: ring_gather(): lax.ppermute(going_down, axis, [(d, (d - 1) % ways) for d in range(ways)])]
  transfers between devices with their start and end apart: 1 -> 5, of which waited for: 1 -> 4; matrix products, arithmetic and copies ran while one was open for 0% -> 0% of each run, Pallas kernels for 0% -> 0%
where the time goes in v1:
time: 201 us; the launch traced here: 200 us
  blocking collectives  133 us (66%)
  waiting for transfers between devices  26.3 us (13%)
  matrix products  13.3 us (7%)
  starting transfers between devices  11.4 us (6%)
  local copies, waits for them, and re-layouts  8.02 us (4%)
  other arithmetic  7.12 us (4%)
    all_to_all x1, blocking collectives, on_device(): lax.all_to_all(new_momentum, 'shard', split_axis=0, concat_axis=1, tiled=...  63.1 us
    all_to_all x1, blocking collectives, on_device(): lax.all_to_all(rows, 'shard', split_axis=1, concat_axis=0, tiled=True)  57.6 us
    all_to_all x2, waiting for transfers between devices, summed_gram(): lax.all_to_all(part, 'model', split_axis=0, concat_axis=0, tiled=True)  17.2 us
    all_gather x1, blocking collectives, on_device(): rows = mul(lax.all_gather(first, 'model', axis=0, tiled=True), rows)  12.8 us
    ppermute x2, waiting for transfers between devices, ring_gather(): lax.ppermute(going_up, axis, [(d, (d + 1) % ways) for d in range(ways)])  9.07 us
    all_to_all x2, starting transfers between devices, summed_gram(): lax.all_to_all(part, 'model', split_axis=0, concat_axis=0, tiled=True)  8.12 us
    dot_general x16, matrix products, mul(): return jnp.einsum('mij,mjk->mik', a, b, precision=HIGH)  7.57 us
    dot_general x2, matrix products, summed_gram(): part = jnp.einsum('mik,mjk->mij', rows, rows, precision=HIGH)  5.72 us
  transfers between devices with their start and end apart: 5, of which 4 were waited for; matrix products, arithmetic and copies ran while one was open for 0% of the time, Pallas kernels for 0%

profile of v1, /device:TPU:2, one launch (start us, length us, event | category | flops | bytes accessed | tf_op | source)
XLA Modules:
  0.0 200.5 jit_solution(3712491907873789845)
XLA Ops:
  0.6 3.7 %multiply_add_fusion = f32[512,2,512]{2,1,0:T(2,128)S(1)} fusion(f32[512,2,512]{2,1,0:T(2,128)} %param.3, f32[512,2,512]{2,1,0:T(2,128)} %param.4), kind=kLoop, calls=%fused_computation.2 | loop fusion | flops 1048576 | bytes 6291456 | tf_op jit(solution)/shard_map/add | solution.py:52
  4.3 63.1 %all_to_all.46 = f32[512,2,512]{2,1,0:T(2,128)S(1)} all-to-all(f32[512,2,512]{2,1,0:T(2,128)S(1)} %multiply_add_fusion), channel_id=1, replica_groups=mesh['shard'=64,'model'=4] {'shard'}, dimensions={0} | all-to-all | bytes 4194304 | tf_op jit(solution)/shard_map/all_to_all | solution.py:53
  67.4 2.1 %copy.11 = f32[64,8,2,512]{3,2,0,1:T(2,128)} copy(f32[64,8,2,512]{3,2,1,0:T(2,128)S(1)} %bitcast.46) | data formatting | bytes 4194304 | tf_op jit(solution)/shard_map/all_to_all | solution.py:53
  69.4 2.7 %all_to_all.35 = f32[8,128,512]{2,1,0:T(8,128)S(1)} reshape(f32[8,64,2,512]{3,2,1,0:T(2,128)} %bitcast.44) | data formatting | bytes 4194304 | tf_op jit(solution)/shard_map/all_to_all | solution.py:53
  72.2 2.9 %fusion.8 = f32[8,128,128]{2,1,0:T(8,128)} fusion(f32[8,128,512]{2,1,0:T(8,128)S(1)} %all_to_all.35), kind=kOutput, calls=%fused_computation.26 | convolution fusion | flops 805306368 | bytes 2621440 | tf_op jit(solution)/shard_map/mik,mjk->mij/dot_general | solution.py:46
  75.0 4.5 %all-to-all-start.1 = ((f32[8,128,128]{2,1,0:T(8,128)}), f32[8,128,128]{2,1,0:T(8,128)S(1)}, u32[]{:S(2)}, u32[]{:S(2)}) async-start(f32[8,128,128]{2,1,0:T(8,128)} %fusion.8), calls=%async_computation.1 | async-start | bytes 1048576 | tf_op jit(solution)/shard_map/all_to_all | solution.py:47
  79.5 8.0 %all-to-all-done.1 = f32[8,128,128]{2,1,0:T(8,128)S(1)} async-done(((f32[8,128,128]{2,1,0:T(8,128)}), f32[8,128,128]{2,1,0:T(8,128)S(1)}, u32[]{:S(2)}, u32[]{:S(2)}) %all-to-all-start.1) | async-done | bytes 524320 | tf_op jit(solution)/shard_map/all_to_all | solution.py:47
  87.7 0.4 fusion.4
  88.1 0.3 fusion.5
  88.4 0.3 fusion.9
  88.7 0.3 fusion.3
  89.0 0.3 convolution_multiply_fusion.3
  89.3 12.8 %all_gather.3 = f32[8,128,128]{2,1,0:T(8,128)S(1)} all-gather(f32[2,128,128]{2,1,0:T(8,128)S(1)} %convolution_multiply_fusion.3), channel_id=1, replica_groups=mesh['shard'=64,'model'=4] {'model'}, dimensions={0}, use_global_device_ids=true | all-gather | bytes 655360 | tf_op jit(solution)/shard_map/all_gather | solution.py:57
  102.1 1.8 fusion.10
  103.9 2.9 %fusion.11 = f32[8,128,128]{2,1,0:T(8,128)} fusion(f32[8,128,512]{2,1,0:T(8,128)S(1)} %fusion.10), kind=kOutput, calls=%fused_computation.29 | convolution fusion | flops 805306368 | bytes 2621440 | tf_op jit(solution)/shard_map/mik,mjk->mij/dot_general | solution.py:46
  106.8 3.7 %all-to-all-start.2 = ((f32[8,128,128]{2,1,0:T(8,128)}), f32[8,128,128]{2,1,0:T(8,128)S(1)}, u32[]{:S(2)}, u32[]{:S(2)}) async-start(f32[8,128,128]{2,1,0:T(8,128)} %fusion.11), calls=%async_computation.2 | async-start | bytes 1048576 | tf_op jit(solution)/shard_map/all_to_all | solution.py:47
  110.4 9.2 %all-to-all-done.2 = f32[8,128,128]{2,1,0:T(8,128)S(1)} async-done(((f32[8,128,128]{2,1,0:T(8,128)}), f32[8,128,128]{2,1,0:T(8,128)S(1)}, u32[]{:S(2)}, u32[]{:S(2)}) %all-to-all-start.2) | async-done | bytes 524320 | tf_op jit(solution)/shard_map/all_to_all | solution.py:47
  119.9 0.3 fusion.12
  120.2 0.3 fusion.13
  120.4 0.3 fusion.1
  121.0 0.3 fusion.14
  121.3 0.3 fusion.15
  121.5 0.3 fusion
  121.9 0.3 constant_dynamic-update-slice_fusion.3
  122.2 3.2 %collective-permute-start.1 = (f32[2,128,128]{2,1,0:T(8,128)S(1)}, f32[2,128,128]{2,1,0:T(8,128)S(1)}, u32[]{:S(2)}, u32[]{:S(2)}) collective-permute-start(f32[2,128,128]{2,1,0:T(8,128)S(1)} %get-tuple-element.3), channel_id=1, source_target_pairs={{0,3},{1,0},{2,1},{3,2},{4,7},{5,4},{6,5},{7,6},{8,11},{9,8},{10,9... | collective-permute-start | bytes 393224 | tf_op jit(solution)/shard_map/ppermute | solution.py:23
  125.5 2.9 %collective-permute-done = f32[2,128,128]{2,1,0:T(8,128)S(1)} collective-permute-done((f32[2,128,128]{2,1,0:T(8,128)S(1)}, f32[2,128,128]{2,1,0:T(8,128)S(1)}, u32[]{:S(2)}, u32[]{:S(2)}) %collective-permute-start) | collective-permute-done | bytes 131104 | tf_op jit(solution)/shard_map/ppermute | solution.py:20
  128.5 6.1 %collective-permute-done.2 = f32[2,128,128]{2,1,0:T(8,128)S(1)} collective-permute-done((f32[2,128,128]{2,1,0:T(8,128)S(1)}, f32[2,128,128]{2,1,0:T(8,128)S(1)}, u32[]{:S(2)}, u32[]{:S(2)}) %collective-permute-start.2) | collective-permute-done | bytes 131104 | tf_op jit(solution)/shard_map/ppermute | solution.py:20
  134.6 1.8 fusion.17
  136.4 1.2 copy.8
  137.7 57.6 %all_to_all.47 = f32[8,128,512]{2,0,1:T(8,128)S(1)} all-to-all(f32[8,128,512]{2,0,1:T(8,128)S(1)} %copy.8), channel_id=1, replica_groups=mesh['shard'=64,'model'=4] {'shard'}, dimensions={1} | all-to-all | bytes 4194304 | tf_op jit(solution)/shard_map/all_to_all | solution.py:60
  195.3 1.9 copy.9
  197.2 3.3 %bitcast_subtract_fusion = f32[512,2,512]{2,1,0:T(2,128)} fusion(f32[64,8,2,512]{3,2,1,0:T(2,128)S(1)} %copy.9, f32[512,2,512]{2,1,0:T(2,128)S(1)} %copy-done.3), kind=kLoop, calls=%fused_computation | loop fusion | flops 1048576 | bytes 6291456 | tf_op jit(solution)/shard_map/sub | solution.py:61
  (23 shorter events, 0.9 us)
Async XLA Ops:
  4.3 63.1 %copy-start.2 = (f32[512,2,512]{2,1,0:T(2,128)}, f32[512,2,512]{2,1,0:T(2,128)S(1)}, u32[]{:S(2)}) copy-start(f32[512,2,512]{2,1,0:T(2,128)S(1)} %multiply_add_fusion) | copy-start | bytes 6291460
  72.1 2.9 %copy-start = (f32[8,128,512]{2,1,0:T(8,128)}, f32[8,128,512]{2,1,0:T(8,128)S(1)}, u32[]{:S(2)}) copy-start(f32[8,128,512]{2,1,0:T(8,128)S(1)} %all_to_all.35) | copy-start | bytes 6291460
  75.0 12.5 %all-to-all-start.1 = ((f32[8,128,128]{2,1,0:T(8,128)}), f32[8,128,128]{2,1,0:T(8,128)S(1)}, u32[]{:S(2)}, u32[]{:S(2)}) async-start(f32[8,128,128]{2,1,0:T(8,128)} %fusion.8), calls=%async_computation.1 | async-start | bytes 1048576 | tf_op jit(solution)/shard_map/all_to_all | solution.py:47
  87.6 14.5 %copy-start.1 = (f32[8,128,512]{2,1,0:T(8,128)S(1)}, f32[8,128,512]{2,1,0:T(8,128)}, u32[]{:S(2)}) copy-start(f32[8,128,512]{2,1,0:T(8,128)} %copy-done) | copy-start | bytes 6291460
  106.8 12.8 %all-to-all-start.2 = ((f32[8,128,128]{2,1,0:T(8,128)}), f32[8,128,128]{2,1,0:T(8,128)S(1)}, u32[]{:S(2)}, u32[]{:S(2)}) async-start(f32[8,128,128]{2,1,0:T(8,128)} %fusion.11), calls=%async_computation.2 | async-start | bytes 1048576 | tf_op jit(solution)/shard_map/all_to_all | solution.py:47
  122.1 6.3 %collective-permute-start = (f32[2,128,128]{2,1,0:T(8,128)S(1)}, f32[2,128,128]{2,1,0:T(8,128)S(1)}, u32[]{:S(2)}, u32[]{:S(2)}) collective-permute-start(f32[2,128,128]{2,1,0:T(8,128)S(1)} %get-tuple-element.3), channel_id=1, source_target_pairs={{0,1},{1,2},{2,3},{3,0},{4,5},{5,6},{6,7},{7,4},{8,9},{9,10},{10,1... | collective-permute-start | bytes 393224 | tf_op jit(solution)/shard_map/ppermute | solution.py:20
  122.2 6.2 %collective-permute-start.1 = (f32[2,128,128]{2,1,0:T(8,128)S(1)}, f32[2,128,128]{2,1,0:T(8,128)S(1)}, u32[]{:S(2)}, u32[]{:S(2)}) collective-permute-start(f32[2,128,128]{2,1,0:T(8,128)S(1)} %get-tuple-element.3), channel_id=1, source_target_pairs={{0,3},{1,0},{2,1},{3,2},{4,7},{5,4},{6,5},{7,6},{8,11},{9,8},{10,9... | collective-permute-start | bytes 393224 | tf_op jit(solution)/shard_map/ppermute | solution.py:23
  128.4 6.2 %collective-permute-start.2 = (f32[2,128,128]{2,1,0:T(8,128)S(1)}, f32[2,128,128]{2,1,0:T(8,128)S(1)}, u32[]{:S(2)}, u32[]{:S(2)}) collective-permute-start(f32[2,128,128]{2,1,0:T(8,128)S(1)} %collective-permute-done), channel_id=1, source_target_pairs={{0,1},{1,2},{2,3},{3,0},{4,5},{5,6},{6,7},{7,4},{8,9},{9,10},{10,1... | collective-permute-start | bytes 393224 | tf_op jit(solution)/shard_map/ppermute | solution.py:20
  195.3 1.9 copy-start.3
